TPU v7x, 8 devices: a whole 2x2x1 slice. The times are simulated.
8 devices in a mesh: dp: 1 (over z), tp: 8 (over x, y, core).
Axes of the slice: x: 2, y: 2, z: 1, core: 2. Of those that a mesh axis runs over, the one named last changes fastest.
Arguments:
- x: bfloat16 [64, 2048], P('dp')
- k_cache: bfloat16 [64, 4096, 32, 64], P('dp', None, 'tp')
- v_cache: bfloat16 [64, 4096, 32, 64], P('dp', None, 'tp')
- gain_a: bfloat16 [2048], replicated
- wq: bfloat16 [2048, 2048], P(None, 'tp')
- wo: bfloat16 [2048, 2048], P('tp')
- gain_m: bfloat16 [2048], replicated
- w_gate: bfloat16 [2048, 5120], P(None, 'tp')
- w_up: bfloat16 [2048, 5120], P(None, 'tp')
- w_down: bfloat16 [5120, 2048], P('tp')
Outputs:
- output: bfloat16 [64, 2048], P('dp')
All inputs are finite; a program needn't handle non-finite values.
Results may differ from a plain program's by a relative error of at most 0.017.
Values are sent between devices in bfloat16 or wider.
A program may use at most 2 GiB of HBM per device.

v0:
```python
import jax
import jax.numpy as jnp
from jax import lax
from jax.sharding import PartitionSpec as P

HEAD = 64
THETA = 10000


def normed(x, gain):
    wide = x.astype(jnp.float32)
    scale = lax.rsqrt(jnp.mean(wide * wide, -1, keepdims=True) + 1e-6)
    return (wide * scale * gain.astype(jnp.float32)).astype(jnp.bfloat16)


def turned(t, place, theta):
    half = t.shape[-1] // 2
    angle = place.astype(jnp.float32)[:, None] * theta ** (-jnp.arange(half, dtype=jnp.float32) / half)
    cos, sin = jnp.cos(angle)[:, None], jnp.sin(angle)[:, None]
    a, b = t[..., :half].astype(jnp.float32), t[..., half:].astype(jnp.float32)
    return jnp.concatenate([a * cos - b * sin, b * cos + a * sin], -1).astype(jnp.bfloat16)


def matmul(a, w):
    return jnp.dot(a, w, preferred_element_type=jnp.float32).astype(jnp.bfloat16)


def einsum(form, a, b):
    return jnp.einsum(form, a.astype(jnp.float32), b.astype(jnp.float32))


def seen_by(a, wq, k_cache, v_cache, head, theta):
    batch, cache, kv_heads = k_cache.shape[:3]
    place = jnp.full((batch,), cache - 1)
    q = turned(matmul(a, wq).reshape(batch, -1, head), place, theta).reshape(batch, kv_heads, -1, head)
    scores = einsum("bgsd,bugd->bgsu", q, k_cache) * head**-0.5
    weights = jax.nn.softmax(scores, -1).astype(jnp.bfloat16)
    return einsum("bgsu,bugd->bgsd", weights, v_cache).astype(jnp.bfloat16).reshape(batch, -1)


def hidden_of(b, w_gate, w_up):
    gate = jnp.dot(b, w_gate, preferred_element_type=jnp.float32)
    up = jnp.dot(b, w_up, preferred_element_type=jnp.float32)
    return (jax.nn.silu(gate) * up).astype(jnp.bfloat16)


def solution(mesh):
    def added(t, term):
        return (t.astype(jnp.float32) + lax.psum(term.astype(jnp.bfloat16), "tp").astype(jnp.float32)).astype(jnp.bfloat16)

    def step(x, k_cache, v_cache, gain_a, wq, wo, gain_m, w_gate, w_up, w_down):
        seen = seen_by(normed(x, gain_a), wq, k_cache, v_cache, HEAD, THETA)
        h = added(x, jnp.dot(seen, wo, preferred_element_type=jnp.float32))
        return added(h, jnp.dot(hidden_of(normed(h, gain_m), w_gate, w_up), w_down, preferred_element_type=jnp.float32))

    states, cache, columns, rows_of = P("dp", None), P("dp", None, "tp", None), P(None, "tp"), P("tp", None)
    return jax.shard_map(
        step,
        mesh=mesh,
        in_specs=(states, cache, cache, P(None), columns, rows_of, P(None), columns, columns, rows_of),
        out_specs=states,
        check_vma=False,
    )
```

profile of v0, /device:TPU:0, one launch (start us, length us, event | category | flops | bytes accessed | tf_op | source)
XLA Modules:
  0.0 223.8 jit_solution(16771499683906850522)
XLA Ops:
  6.5 0.0 copy-start
  6.5 0.0 all-reduce.3.cloned.1.call-start
  6.6 0.8 convert_element_type.66
  7.4 1.1 fusion.12
  8.6 1.7 convolution_convert_fusion.2
  10.2 0.1 copy.11
  10.3 0.1 fusion.34
  10.5 0.1 copy.12
  10.6 43.9 %fusion.45 = f32[64,4,1,4096]{3,2,1,0:T(1,128)} fusion(bf16[64,4,64,1]{2,3,1,0:T(2,128)(2,1)S(1)} %copy.12, bf16[64,4096,4,64]{1,3,2,0:T(8,128)(2,1)} %param.11), kind=kOutput, calls=%fused_computation.58 | convolution fusion | flops 134217728 | bytes 138444800 | tf_op jit(solution)/shard_map/bgsd,bugd->bgsu/dot_general | solution.py:29
  54.5 8.8 %fusion.6 = bf16[64,4,4096,1]{2,0,1,3:T(8,128)(2,1)} fusion(f32[64,4,1,4096]{3,2,1,0:T(1,128)} %fusion.45), kind=kOutput, calls=%fused_computation.6 | output fusion | flops 4203006 | bytes 6291456 | tf_op jit(solution)/shard_map/div | solution.py:37
  63.2 0.0 copy-start.2
  63.2 0.0 copy-start.1
  63.2 54.9 %fusion.7 = f32[64,4,1,64]{3,2,1,0:T(1,128)S(1)} fusion(bf16[64,4096,4,64]{1,3,2,0:T(8,128)(2,1)} %param.12, bf16[64,4,4096,1]{2,0,1,3:T(8,128)(2,1)} %fusion.6), kind=kOutput, calls=%fused_computation.8 | convolution fusion | flops 134217728 | bytes 136380416 | tf_op jit(solution)/shard_map/bgsu,bugd->bgsd/dot_general | solution.py:29
  118.2 0.1 reshape.62
  118.3 2.2 convolution_convert_fusion.1
  120.5 0.0 all-reduce.3.cloned.1.call-update
  120.5 0.0 all-reduce.5.cloned.1.call-start
  120.6 0.0 copy-done.2
  120.6 45.5 %all-reduce.3.cloned.1.call-done = bf16[64,2048]{1,0:T(8,128)(2,1)} async-done(((bf16[64,2048]{1,0:T(8,128)(2,1)}), bf16[64,2048]{1,0:T(8,128)(2,1)}) %all-reduce.3.cloned.1.call-update) | async-done | bytes 262160 | tf_op jit(solution)/shard_map/psum | solution.py:49
  166.1 0.0 copy-done.1
  166.1 1.1 fusion.16
  167.3 2.4 %fusion.31 = f32[64,640]{1,0:T(8,128)S(1)} fusion(bf16[2048,640]{1,0:T(8,128)(2,1)} %param.17, bf16[64,2048]{1,0:T(8,128)(2,1)S(1)} %get-tuple-element.6, f32[2048]{0:T(1024)S(1)} %convert_element_type.77, f32[64]{0:T(128)S(1)} %add_rsqrt_fusion), kind=kOutput, calls=%fused_computation.43 | convolution fusion | flops 168296448 | bytes 3055872 | tf_op jit(solution)/shard_map/dot_general | solution.py:42
  169.6 0.0 copy-done
  169.6 3.6 %convolution_convert_fusion = bf16[64,2048]{1,0:T(8,128)(2,1)} fusion(bf16[640,2048]{1,0:T(8,128)(2,1)S(1)} %copy-done, bf16[2048,640]{1,0:T(8,128)(2,1)} %param.18, f32[64,640]{1,0:T(8,128)S(1)} %fusion.31, bf16[64,2048]{1,0:T(8,128)(2,1)S(1)} %get-tuple-element.6, f32[2048]{0:T(1024)S(1)} %convert_element_type.77, f32[64]{0:T(128)S(1)} %add_rsqrt_fusion), kind=kOutput, calls=%fused_computation.11 | convolution fusion | flops 336445440 | bytes 5939456 | tf_op jit(solution)/shard_map/dot_general | solution.py:54
  173.2 0.0 all-reduce.5.cloned.1.call-update
  173.2 42.0 %all-reduce.5.cloned.1.call-done = bf16[64,2048]{1,0:T(8,128)(2,1)} async-done(((bf16[64,2048]{1,0:T(8,128)(2,1)}), bf16[64,2048]{1,0:T(8,128)(2,1)}) %all-reduce.5.cloned.1.call-update) | async-done | bytes 262160 | tf_op jit(solution)/shard_map/psum | solution.py:49
  215.3 1.7 fusion.19
  (6 shorter events, 0.1 us)
Async XLA Ops:
  6.5 163.1 %copy-start = (bf16[640,2048]{1,0:T(8,128)(2,1)S(1)}, bf16[640,2048]{1,0:T(8,128)(2,1)}, u32[]{:S(2)}) copy-start(bf16[640,2048]{1,0:T(8,128)(2,1)} %param.19) | copy-start | bytes 7864324
  6.5 159.6 %all-reduce.3.cloned.1.call-start = ((), (), s32[]{:S(2)}) async-start(), calls=%async_computation | async-start | bytes 524288 | tf_op jit(solution)/shard_map/psum | solution.py:49
  63.2 57.4 %copy-start.2 = (bf16[2048]{0:T(1024)(128)(2,1)S(1)}, bf16[2048]{0:T(1024)(128)(2,1)}, u32[]{:S(2)}) copy-start(bf16[2048]{0:T(1024)(128)(2,1)} %param.16) | copy-start | bytes 12292
  63.2 102.9 %copy-start.1 = (bf16[64,2048]{1,0:T(8,128)(2,1)S(1)}, bf16[64,2048]{1,0:T(8,128)(2,1)}, u32[]{:S(2)}) copy-start(bf16[64,2048]{1,0:T(8,128)(2,1)} %param.10) | copy-start | bytes 786436
  120.5 94.7 %all-reduce.5.cloned.1.call-start = ((), (), s32[]{:S(2)}) async-start(), calls=%async_computation.1 | async-start | bytes 524288 | tf_op jit(solution)/shard_map/psum | solution.py:49
Sparse Core Ops, SparseCore 0:
  120.7 45.3 all-reduce.2
  173.3 41.8 all-reduce.4
where the time goes:
time: 224 us
  matrix products  109 us (49%)
  waiting for transfers between devices  87.6 us (39%)
  other arithmetic  13.8 us (6%)
  between operations  13.5 us (6%)
    dot_general x2, matrix products, einsum(): return jnp.einsum(form, a.astype(jnp.float32), b.astype(jnp.float32))  98.8 us
    psum x2, waiting for transfers between devices, added(): lax.psum(term.astype(jnp.bfloat16), 'tp').astype(jnp.float32)  87.5 us
    div x1, other arithmetic, seen_by(): weights = jax.nn.softmax(scores, -1).astype(jnp.bfloat16)  8.77 us
  transfers between devices with their start and end apart: 2, of which 2 were waited for; matrix products, arithmetic and copies ran while one was open for 0% of the time, Pallas kernels for 0%

commit v1 on v0

v1 whole, which is shorter than its diff:
```python
import functools

import jax
import jax.numpy as jnp
import numpy as np
from jax import lax
from jax.experimental import pallas as pl
from jax.experimental.pallas import tpu as pltpu
from jax.sharding import PartitionSpec as P

HEAD = 64
THETA = 10000
EPS = 1e-6
SLOTS = 10
CHUNKS = (16, 16, 16, 8, 8)
MESH = pl.DeviceIdType.MESH
F32, BF16 = jnp.float32, jnp.bfloat16


def turn_table(place, heads):
    half = HEAD // 2
    angle = np.float32(place) * np.float32(THETA) ** (-np.arange(half, dtype=np.float32) / np.float32(half))
    angle = angle.astype(np.float32)
    cos, sin = np.cos(angle), np.sin(angle)
    return np.stack([np.tile(np.concatenate([cos, cos]), heads), np.tile(np.concatenate([-sin, sin]), heads)]).astype(np.float32)


def dot(a, b):
    return jnp.dot(a, b, preferred_element_type=F32)


def dot_t(a, b):
    return lax.dot_general(a, b, (((1,), (1,)), ((), ())), preferred_element_type=F32)


def normed(wide, gain):
    return (wide * lax.rsqrt(jnp.mean(wide * wide, -1, keepdims=True) + EPS) * gain).astype(BF16)


def kernel(n, k_hbm, v_hbm, x_hbm, ga_hbm, wq_hbm, wo_hbm, gm_hbm, wg_hbm, wu_hbm, wd_hbm, table_hbm, y_ref, *scratch):
    rows, width, cache = k_hbm.shape
    heads = width // HEAD
    hidden = wg_hbm.shape[1]
    (kbuf, vbuf, x_ref, ga, gm, table, wq, wo, wgu, wd, xf, hf, qf, seen, scores, ksem, vsem, wsem) = scratch[:18]
    chunks = len(CHUNKS)
    first, second = scratch[18 : 18 + chunks], scratch[18 + chunks : 18 + 2 * chunks]
    send_sem, recv_sem = scratch[18 + 2 * chunks :]
    me = lax.axis_index("tp")
    peers = [lax.rem(me + i, n) for i in range(1, n)]

    def kcopy(s):
        slot = lax.rem(s, SLOTS)
        return pltpu.make_async_copy(k_hbm.at[s], kbuf.at[slot], ksem.at[slot])

    def vcopy(s):
        slot = lax.rem(s, SLOTS)
        return pltpu.make_async_copy(v_hbm.at[s], vbuf.at[slot], vsem.at[slot])

    small = [
        pltpu.make_async_copy(src, dst, wsem.at[i])
        for i, (src, dst) in enumerate(
            [
                (x_hbm, x_ref),
                (ga_hbm, ga),
                (wq_hbm, wq),
                (table_hbm, table),
                (wo_hbm, wo),
                (gm_hbm, gm),
                (wg_hbm, wgu.at[:, :hidden]),
                (wu_hbm, wgu.at[:, hidden:]),
                (wd_hbm, wd),
            ]
        )
    ]
    for copy in small[:4]:
        copy.start()
    for s in range(SLOTS):
        kcopy(s).start()
        vcopy(s).start()
    for copy in small[4:]:
        copy.start()

    barrier = pltpu.get_barrier_semaphore()
    for peer in peers:
        pl.semaphore_signal(barrier, inc=1, device_id={"tp": peer}, device_id_type=MESH)

    for copy in small[:2]:
        copy.wait()
    xf[...] = x_ref[...].astype(F32)
    a = normed(xf[...], ga[...].astype(F32))
    for copy in small[2:4]:
        copy.wait()
    q = dot(a, wq[...]).astype(BF16).astype(F32)
    half = HEAD // 2
    lane = lax.broadcasted_iota(jnp.int32, q.shape, 1)
    other = jnp.where(lax.rem(lane, HEAD) < half, pltpu.roll(q, width - half, 1), pltpu.roll(q, half, 1))
    qf[...] = (q * table[0:1, :] + other * table[1:2, :]).astype(BF16).astype(F32)

    own = lax.broadcasted_iota(jnp.int32, (8, width), 1) // HEAD == lax.broadcasted_iota(jnp.int32, (8, width), 0)

    def score(s):
        query = jnp.where(own, jnp.broadcast_to(qf[pl.ds(s, 1), :], (8, width)), 0.0).astype(BF16)
        return dot(query, kbuf[lax.rem(s, SLOTS)])

    def attend(s, wide):
        scaled = wide * HEAD**-0.5
        e = jnp.exp(scaled - jnp.max(scaled, -1, keepdims=True))
        weights = (e * (1.0 / jnp.sum(e, -1, keepdims=True))).astype(BF16)
        out = dot_t(weights, vbuf[lax.rem(s, SLOTS)])
        seen[pl.ds(s, 1), :] = jnp.sum(jnp.where(own, out, 0.0), 0, keepdims=True)

    def step(s, _):
        kcopy(s + 1).wait()
        vcopy(s).wait()
        wide = scores[lax.rem(s, 2)]
        scores[lax.rem(s + 1, 2)] = score(s + 1)
        attend(s, wide)

        @pl.when(s + 1 + SLOTS < rows)
        def _():
            kcopy(s + 1 + SLOTS).start()

        @pl.when(s + SLOTS < rows)
        def _():
            vcopy(s + SLOTS).start()

        return 0

    def sends(half, c, buf):
        return [
            pltpu.make_async_remote_copy(
                src_ref=buf.at[me],
                dst_ref=buf.at[me],
                send_sem=send_sem.at[half, c, i],
                recv_sem=recv_sem.at[half, c, me],
                device_id={"tp": peer},
                device_id_type=MESH,
            )
            for i, peer in enumerate(peers)
        ]

    def receive(half, c, buf):
        for peer in peers:
            pltpu.make_async_remote_copy(
                src_ref=buf.at[peer],
                dst_ref=buf.at[peer],
                send_sem=send_sem.at[half, c, 0],
                recv_sem=recv_sem.at[half, c, peer],
                device_id={"tp": peer},
                device_id_type=MESH,
            ).wait_recv()
        total = buf[0].astype(F32)
        for i in range(1, n):
            total = total + buf[i].astype(F32)
        return total

    starts = [sum(CHUNKS[:c]) for c in range(chunks)]

    def project(c):
        part = slice(starts[c], starts[c] + CHUNKS[c])
        first[c][me] = dot(seen[part, :].astype(BF16), wo[...]).astype(BF16)
        for copy in sends(0, c, first[c]):
            copy.start()

    def feed(c):
        part = slice(starts[c], starts[c] + CHUNKS[c])
        h = (xf[part, :] + receive(0, c, first[c])).astype(BF16).astype(F32)
        hf[part, :] = h
        b = normed(h, gm[...].astype(F32))
        both = dot(b, wgu[...])
        gate, up = both[:, :hidden], both[:, hidden:]
        product = (gate * (1.0 / (1.0 + jnp.exp(-gate))) * up).astype(BF16)
        second[c][me] = dot(product, wd[...]).astype(BF16)
        for copy in sends(1, c, second[c]):
            copy.start()

    def finish(c):
        part = slice(starts[c], starts[c] + CHUNKS[c])
        y_ref[part, :] = (hf[part, :] + receive(1, c, second[c])).astype(BF16)

    kcopy(0).wait()
    scores[0] = score(0)
    for name in [0]:
        kcopy(SLOTS).start()
    for c in range(chunks):
        last = c == chunks - 1
        lax.fori_loop(starts[c], starts[c] + CHUNKS[c] - last, step, 0)
        if last:
            vcopy(rows - 1).wait()
            attend(rows - 1, scores[(rows - 1) % 2])
        if c == 0:
            for copy in small[4:]:
                copy.wait()
            pl.semaphore_wait(barrier, n - 1)
        project(c)
        if c >= 1:
            feed(c - 1)
        if c >= 2:
            finish(c - 2)
    feed(chunks - 1)
    finish(chunks - 2)
    finish(chunks - 1)
    for c in range(chunks):
        for half, buf in ((0, first[c]), (1, second[c])):
            for copy in sends(half, c, buf):
                copy.wait_send()


def solution(mesh):
    n = mesh.shape["tp"]

    def step(x, k_cache, v_cache, gain_a, wq, wo, gain_m, w_gate, w_up, w_down):
        rows, cache, heads, head = k_cache.shape
        d, width, hidden = x.shape[1], heads * head, w_gate.shape[1]
        flat = lambda t: t.transpose(0, 2, 3, 1).reshape(rows, width, cache)
        table = jnp.asarray(turn_table(cache - 1, heads))
        chunks = len(CHUNKS)
        scratch = [
            pltpu.VMEM((SLOTS, width, cache), BF16),
            pltpu.VMEM((SLOTS, width, cache), BF16),
            pltpu.VMEM((rows, d), BF16),
            pltpu.VMEM((1, d), BF16),
            pltpu.VMEM((1, d), BF16),
            pltpu.VMEM((2, width), F32),
            pltpu.VMEM((d, width), BF16),
            pltpu.VMEM((width, d), BF16),
            pltpu.VMEM((d, 2 * hidden), BF16),
            pltpu.VMEM((hidden, d), BF16),
            pltpu.VMEM((rows, d), F32),
            pltpu.VMEM((rows, d), F32),
            pltpu.VMEM((rows, width), F32),
            pltpu.VMEM((rows, width), F32),
            pltpu.VMEM((2, 8, cache), F32),
            pltpu.SemaphoreType.DMA((SLOTS,)),
            pltpu.SemaphoreType.DMA((SLOTS,)),
            pltpu.SemaphoreType.DMA((9,)),
            *[pltpu.VMEM((n, size, d), BF16) for size in CHUNKS],
            *[pltpu.VMEM((n, size, d), BF16) for size in CHUNKS],
            pltpu.SemaphoreType.DMA((2, chunks, n - 1)),
            pltpu.SemaphoreType.DMA((2, chunks, n)),
        ]
        return pl.pallas_call(
            functools.partial(kernel, n),
            out_shape=jax.ShapeDtypeStruct((rows, d), BF16),
            in_specs=[pl.BlockSpec(memory_space=pl.ANY)] * 11,
            out_specs=pl.BlockSpec(memory_space=pltpu.VMEM),
            scratch_shapes=scratch,
            compiler_params=pltpu.CompilerParams(collective_id=0, has_side_effects=True, vmem_limit_bytes=65_000_000),
        )(flat(k_cache), flat(v_cache), x, gain_a.reshape(1, d), wq, wo, gain_m.reshape(1, d), w_gate, w_up, w_down, table)

    states, cache, columns, rows_of = P("dp", None), P("dp", None, "tp", None), P(None, "tp"), P("tp", None)
    return jax.shard_map(
        step,
        mesh=mesh,
        in_specs=(states, cache, cache, P(None), columns, rows_of, P(None), columns, columns, rows_of),
        out_specs=states,
        check_vma=False,
    )
```

time: 224 us -> 107 us (0.48)
  matrix products: 109 us -> 0 us
  Pallas kernels: 0 us -> 102 us
  waiting for transfers between devices: 87.6 us -> 0 us
  other arithmetic: 13.8 us -> 0 us
  between operations: 13.5 us -> 0.01 us
  local copies, waits for them, and re-layouts: 0.37 us -> 4.24 us
    dot_general x6 -> x0, matrix products: 109 us -> none  [the longest x2 98.8 us: einsum(): return jnp.einsum(form, a.astype(jnp.float32), b.astype(jnp.float32))]
    pallas_call x0 -> x1, Pallas kernels: none -> 102 us  [step(): pl.pallas_call(functools.partial(kernel, n), out_shape=jax.ShapeDtypeStru...]
    psum x2 -> x0, waiting for transfers between devices: 87.5 us -> none  [added(): lax.psum(term.astype(jnp.bfloat16), 'tp').astype(jnp.float32)]
    div x1 -> x0, other arithmetic: 8.77 us -> none  [seen_by(): weights = jax.nn.softmax(scores, -1).astype(jnp.bfloat16)]
    convert_element_type x4 -> x0, other arithmetic: 2.59 us -> none  [the longest x1 1.71 us: added(): (t.astype(jnp.float32) + lax.psum(term.astype(jnp.bfloat16), 'tp').astype...]
    reshape x1 -> x2, local copies, waits for them, and re-layouts: 0.11 us -> 2.57 us  [the longest x1 1.29 us: step(): gain_a.reshape(1, d)]
    reduce_sum x2 -> x0, other arithmetic: 2.24 us -> none  [normed(): scale = lax.rsqrt(jnp.mean(wide * wide, -1, keepdims=True) + 1e-06)]
  transfers between devices with their start and end apart: 2 -> 0, of which waited for: 2 -> 0; matrix products, arithmetic and copies ran while one was open for 0% -> 0% of each run, Pallas kernels for 0% -> 0%
where the time goes in v1:
time: 107 us
  Pallas kernels  102 us (95%)
  local copies, waits for them, and re-layouts  4.24 us (4%)
    pallas_call x1, Pallas kernels, step(): pl.pallas_call(functools.partial(kernel, n), out_shape=jax.ShapeDtypeStru...  102 us

profile of v1, /device:TPU:0, one launch (start us, length us, event | category | flops | bytes accessed | tf_op | source)
XLA Modules:
  0.0 106.6 jit_solution(3174895655969213246)
XLA Ops:
  0.0 1.3 %reshape.14.ga_hbm = bf16[1,2048]{1,0:T(2,128)(2,1)} reshape(bf16[2048]{0:T(1024)(128)(2,1)} %param.14) | data formatting | bytes 8192 | tf_op jit(solution)/shard_map/reshape | solution.py:249
  1.3 1.3 %reshape.15.gm_hbm = bf16[1,2048]{1,0:T(2,128)(2,1)} reshape(bf16[2048]{0:T(1024)(128)(2,1)} %param.17) | data formatting | bytes 8192 | tf_op jit(solution)/shard_map/reshape | solution.py:249
  2.6 102.3 %shard_map.109 = bf16[64,2048]{1,0:T(8,128)(2,1)} custom-call(bf16[64,256,4096]{2,1,0:T(8,128)(2,1)} %bitcast.1.k_hbm, bf16[64,256,4096]{2,1,0:T(8,128)(2,1)} %bitcast.3.v_hbm, bf16[64,2048]{1,0:T(8,128)(2,1)} %x_hbm.1, bf16[1,2048]{1,0:T(2,128)(2,1)} %reshape.14.ga_hbm, bf16[2048,256]{1,0:T(8,128)(2,1)} %wq_hbm.1, bf16[256,2048]{1,0:T(8,128)(2,1)} %wo_hbm.1, ...), custom_call_target="tpu_custom_call" | custom-call | tf_op jit(solution)/shard_map/pallas_call | solution.py:242
  104.9 1.7 %copy.13 = bf16[64,2048]{1,0:T(8,128)(2,1)} copy(bf16[64,2048]{1,0:T(8,128)(2,1)} %shard_map.109) | data formatting | bytes 524288

commit v2 on v1

v2 whole, which is shorter than its diff:
```python
import functools

import jax
import jax.numpy as jnp
import numpy as np
from jax import lax
from jax.experimental import pallas as pl
from jax.experimental.pallas import tpu as pltpu
from jax.sharding import PartitionSpec as P

HEAD = 64
THETA = 10000
EPS = 1e-6
SLOTS = 8
CHUNKS = ((32, True), (20, True), (8, False), (4, False))
EVENTS = (
    (32, (("project", 0),)),
    (36, (("reduce1", 0),)),
    (40, (("feed", 0),)),
    (44, (("reduce2", 0),)),
    (48, (("finish", 0),)),
    (52, (("project", 1),)),
    (54, (("reduce1", 1),)),
    (58, (("feed", 1),)),
    (60, (("project", 2),)),
    (64, (("project", 3), ("reduce2", 1), ("feed", 2), ("feed", 3), ("finish", 1), ("finish", 2), ("finish", 3))),
)
MESH = pl.DeviceIdType.MESH
F32, BF16 = jnp.float32, jnp.bfloat16


def turn_table(place, heads):
    half = HEAD // 2
    angle = np.float32(place) * np.float32(THETA) ** (-np.arange(half, dtype=np.float32) / np.float32(half))
    angle = angle.astype(np.float32)
    cos, sin = np.cos(angle), np.sin(angle)
    return np.stack([np.tile(np.concatenate([cos, cos]), heads), np.tile(np.concatenate([-sin, sin]), heads)]).astype(np.float32)


def dot(a, b):
    return jnp.dot(a, b, preferred_element_type=F32)


def dot_t(a, b):
    return lax.dot_general(a, b, (((1,), (1,)), ((), ())), preferred_element_type=F32)


def normed(wide, gain):
    return (wide * lax.rsqrt(jnp.mean(wide * wide, -1, keepdims=True) + EPS) * gain).astype(BF16)


def row_of(ref):
    wide = ref[...].astype(F32)
    return jnp.concatenate([wide[i : i + 1, :] for i in range(wide.shape[0])], 1)


def kernel(n, k_hbm, v_hbm, x_hbm, ga_hbm, wq_hbm, wo_hbm, gm_hbm, wg_hbm, wu_hbm, wd_hbm, table_hbm, y_ref, *scratch):
    rows, width, cache = k_hbm.shape
    heads = width // HEAD
    hidden = wg_hbm.shape[1]
    (kbuf, vbuf, x_ref, ga, gm, table, wq, wo, wgu, wd, xf, hf, qf, seen, scores, ksem, vsem, wsem) = scratch[:18]
    chunks = len(CHUNKS)
    send_sem, recv_sem = scratch[18:20]
    rest, bufs = list(scratch[20:]), []
    for _, split in CHUNKS:
        count = 6 if split else 2
        bufs.append(rest[:count])
        rest = rest[count:]
    me = lax.axis_index("tp")
    peers = [lax.rem(me + i, n) for i in range(1, n)]
    if n == 8:
        x, y, core = me // 4, lax.rem(me // 2, 2), lax.rem(me, 2)
        far = [(1, 1, 0), (1, 1, 1), (1, 0, 0), (0, 1, 0), (1, 0, 1), (0, 1, 1), (0, 0, 1)]
        peers = [lax.rem(x + i, 2) * 4 + lax.rem(y + j, 2) * 2 + lax.rem(core + k, 2) for i, j, k in far]

    def kcopy(s):
        slot = lax.rem(s, SLOTS)
        return pltpu.make_async_copy(k_hbm.at[s], kbuf.at[slot], ksem.at[slot])

    def vcopy(s):
        slot = lax.rem(s, SLOTS)
        return pltpu.make_async_copy(v_hbm.at[s], vbuf.at[slot], vsem.at[slot])

    small = [
        pltpu.make_async_copy(src, dst, wsem.at[i])
        for i, (src, dst) in enumerate(
            [
                (x_hbm, x_ref),
                (ga_hbm, ga),
                (wq_hbm, wq),
                (table_hbm, table),
                (wo_hbm, wo),
                (gm_hbm, gm),
                (wg_hbm, wgu.at[:, :hidden]),
                (wu_hbm, wgu.at[:, hidden:]),
                (wd_hbm, wd),
            ]
        )
    ]
    for copy in small[:4]:
        copy.start()
    for s in range(SLOTS):
        kcopy(s).start()
        vcopy(s).start()
    for copy in small[4:]:
        copy.start()

    barrier = pltpu.get_barrier_semaphore()
    for peer in peers:
        pl.semaphore_signal(barrier, inc=1, device_id={"tp": peer}, device_id_type=MESH)

    for copy in small[:2]:
        copy.wait()
    xf[...] = x_ref[...].astype(F32)
    a = normed(xf[...], row_of(ga))
    for copy in small[2:4]:
        copy.wait()
    q = dot(a, wq[...]).astype(BF16).astype(F32)
    half = HEAD // 2
    lane = lax.broadcasted_iota(jnp.int32, q.shape, 1)
    other = jnp.where(lax.rem(lane, HEAD) < half, pltpu.roll(q, width - half, 1), pltpu.roll(q, half, 1))
    qf[...] = (q * table[0:1, :] + other * table[1:2, :]).astype(BF16).astype(F32)

    own = lax.broadcasted_iota(jnp.int32, (8, width), 1) // HEAD == lax.broadcasted_iota(jnp.int32, (8, width), 0)

    def score(s):
        query = jnp.where(own, jnp.broadcast_to(qf[pl.ds(s, 1), :], (8, width)), 0.0).astype(BF16)
        return dot(query, kbuf[lax.rem(s, SLOTS)])

    def attend(s, wide):
        scaled = wide * HEAD**-0.5
        e = jnp.exp(scaled - jnp.max(scaled, -1, keepdims=True))
        weights = (e * (1.0 / jnp.sum(e, -1, keepdims=True))).astype(BF16)
        out = dot_t(weights, vbuf[lax.rem(s, SLOTS)])
        seen[pl.ds(s, 1), :] = jnp.sum(jnp.where(own, out, 0.0), 0, keepdims=True)

    def send(kind, c, i, src, dst):
        return pltpu.make_async_remote_copy(
            src_ref=src,
            dst_ref=dst,
            send_sem=send_sem.at[kind, c, i],
            recv_sem=recv_sem.at[kind, c, me],
            device_id={"tp": peers[i]},
            device_id_type=MESH,
        )

    def arrive(kind, c, buf):
        for peer in peers:
            pltpu.make_async_remote_copy(
                src_ref=buf.at[peer],
                dst_ref=buf.at[peer],
                send_sem=send_sem.at[kind, c, 0],
                recv_sem=recv_sem.at[kind, c, peer],
                device_id={"tp": peer},
                device_id_type=MESH,
            ).wait_recv()

    def total(buf):
        out = buf[0].astype(F32)
        for i in range(1, n):
            out = out + buf[i].astype(F32)
        return out

    def joined(buf):
        return jnp.concatenate([buf[i].astype(F32) for i in range(n)], 1)

    def spread(kind, c, buf):
        return [send(kind, c, i, buf.at[me], buf.at[me]) for i in range(n - 1)]

    def scatter(kind, c, src, dst):
        return [send(kind, c, i, src.at[peers[i]], dst.at[me]) for i in range(n - 1)]

    def start(copies):
        for copy in copies:
            copy.start()

    starts = [sum(size for size, _ in CHUNKS[:c]) for c in range(chunks)]
    parts = [slice(starts[c], starts[c] + CHUNKS[c][0]) for c in range(chunks)]
    tile = x_hbm.shape[1] // n
    mine = pl.ds(pl.multiple_of(me * tile, tile), tile)

    def send_term(half, c, term):
        if CHUNKS[c][1]:
            staged, landed = bufs[c][3 * half], bufs[c][3 * half + 1]
            for i in range(n):
                staged[i] = term[:, i * tile : (i + 1) * tile].astype(BF16)
            start(scatter(2 * half, c, staged, landed))
            landed[me] = staged[me]
        else:
            buf = bufs[c][half]
            buf[me] = term.astype(BF16)
            start(spread(2 * half, c, buf))

    def project(c):
        if c == 0:
            for copy in small[4:]:
                copy.wait()
            pl.semaphore_wait(barrier, n - 1)
        send_term(0, c, dot(seen[parts[c], :].astype(BF16), wo[...]))

    def reduce(half, c):
        landed, whole = bufs[c][3 * half + 1 : 3 * half + 3]
        arrive(2 * half, c, landed)
        before = xf[parts[c], mine] if half == 0 else bufs[c][2][me].astype(F32)
        whole[me] = (before + total(landed)).astype(BF16)
        start(spread(2 * half + 1, c, whole))

    def feed(c):
        if CHUNKS[c][1]:
            arrive(1, c, bufs[c][2])
            h = joined(bufs[c][2])
        else:
            arrive(0, c, bufs[c][0])
            h = (xf[parts[c], :] + total(bufs[c][0])).astype(BF16).astype(F32)
            hf[parts[c], :] = h
        b = normed(h, row_of(gm))
        both = dot(b, wgu[...])
        gate, up = both[:, :hidden], both[:, hidden:]
        product = (gate * (1.0 / (1.0 + jnp.exp(-gate))) * up).astype(BF16)
        send_term(1, c, dot(product, wd[...]))

    def finish(c):
        if CHUNKS[c][1]:
            arrive(3, c, bufs[c][5])
            y_ref[parts[c], :] = joined(bufs[c][5]).astype(BF16)
        else:
            arrive(2, c, bufs[c][1])
            y_ref[parts[c], :] = (hf[parts[c], :] + total(bufs[c][1])).astype(BF16)

    stages = {"project": project, "reduce1": functools.partial(reduce, 0), "feed": feed, "reduce2": functools.partial(reduce, 1), "finish": finish}

    kcopy(0).wait()
    scores[0] = score(0)
    kcopy(SLOTS).start()

    def step(s, _):
        kcopy(s + 1).wait()
        vcopy(s).wait()
        wide = scores[lax.rem(s, 2)]
        scores[lax.rem(s + 1, 2)] = score(s + 1)
        attend(s, wide)

        @pl.when(s + 1 + SLOTS < rows)
        def _():
            kcopy(s + 1 + SLOTS).start()

        @pl.when(s + SLOTS < rows)
        def _():
            vcopy(s + SLOTS).start()

        for row, names in EVENTS:
            if row < rows:

                @pl.when(s == row - 1)
                def _():
                    for name, c in names:
                        stages[name](c)

        return 0

    lax.fori_loop(0, rows - 1, step, 0)
    vcopy(rows - 1).wait()
    attend(rows - 1, scores[(rows - 1) % 2])
    for row, names in EVENTS:
        if row == rows:
            for name, c in names:
                stages[name](c)

    for c in range(chunks):
        for half in range(2):
            if CHUNKS[c][1]:
                copies = scatter(2 * half, c, *bufs[c][3 * half : 3 * half + 2]) + spread(2 * half + 1, c, bufs[c][3 * half + 2])
            else:
                copies = spread(2 * half, c, bufs[c][half])
            for copy in copies:
                copy.wait_send()


def solution(mesh):
    n = mesh.shape["tp"]

    def step(x, k_cache, v_cache, gain_a, wq, wo, gain_m, w_gate, w_up, w_down):
        rows, cache, heads, head = k_cache.shape
        d, width, hidden = x.shape[1], heads * head, w_gate.shape[1]
        flat = lambda t: t.transpose(0, 2, 3, 1).reshape(rows, width, cache)
        table = jnp.asarray(turn_table(cache - 1, heads))
        chunks = len(CHUNKS)
        scratch = [
            pltpu.VMEM((SLOTS, width, cache), BF16),
            pltpu.VMEM((SLOTS, width, cache), BF16),
            pltpu.VMEM((rows, d), BF16),
            pltpu.VMEM((d // 128, 128), BF16),
            pltpu.VMEM((d // 128, 128), BF16),
            pltpu.VMEM((2, width), F32),
            pltpu.VMEM((d, width), BF16),
            pltpu.VMEM((width, d), BF16),
            pltpu.VMEM((d, 2 * hidden), BF16),
            pltpu.VMEM((hidden, d), BF16),
            pltpu.VMEM((rows, d), F32),
            pltpu.VMEM((rows, d), F32),
            pltpu.VMEM((rows, width), F32),
            pltpu.VMEM((rows, width), F32),
            pltpu.VMEM((2, 8, cache), F32),
            pltpu.SemaphoreType.DMA((SLOTS,)),
            pltpu.SemaphoreType.DMA((SLOTS,)),
            pltpu.SemaphoreType.DMA((9,)),
            pltpu.SemaphoreType.DMA((4, chunks, n - 1)),
            pltpu.SemaphoreType.DMA((4, chunks, n)),
        ]
        for size, split in CHUNKS:
            scratch += [pltpu.VMEM((n, size, d // n), BF16)] * 6 if split else [pltpu.VMEM((n, size, d), BF16)] * 2
        return pl.pallas_call(
            functools.partial(kernel, n),
            out_shape=pltpu.VMEM((rows, d), BF16),
            in_specs=[pl.BlockSpec(memory_space=pl.ANY)] * 11,
            out_specs=pl.BlockSpec(memory_space=pltpu.VMEM),
            scratch_shapes=scratch,
            compiler_params=pltpu.CompilerParams(collective_id=0, has_side_effects=True, vmem_limit_bytes=58_000_000),
        )(flat(k_cache), flat(v_cache), x, gain_a.reshape(d // 128, 128), wq, wo, gain_m.reshape(d // 128, 128), w_gate, w_up, w_down, table)

    states, cache, columns, rows_of = P("dp", None), P("dp", None, "tp", None), P(None, "tp"), P("tp", None)
    return jax.shard_map(
        step,
        mesh=mesh,
        in_specs=(states, cache, cache, P(None), columns, rows_of, P(None), columns, columns, rows_of),
        out_specs=states,
        check_vma=False,
    )
```

time: 107 us -> 99.7 us (0.932)
  local copies, waits for them, and re-layouts: 4.24 us -> 0.71 us
  Pallas kernels: 102 us -> 98.9 us
    pallas_call x1, Pallas kernels: 102 us -> 98.9 us  [step(): pl.pallas_call(functools.partial(kernel, n), out_shape=pltpu.VMEM((rows,...]
    reshape x2 -> x0, local copies, waits for them, and re-layouts: 2.57 us -> none  [the longest x1 1.29 us: step(): gain_a.reshape(1, d)]
where the time goes in v2:
time: 99.7 us; the launch traced here: 99.6 us
  Pallas kernels  98.9 us (99%)
    pallas_call x1, Pallas kernels, step(): pl.pallas_call(functools.partial(kernel, n), out_shape=pltpu.VMEM((rows,...  98.9 us

profile of v2, /device:TPU:0, one launch (start us, length us, event | category | flops | bytes accessed | tf_op | source)
XLA Modules:
  0.0 99.6 jit_solution(10877310496934737647)
XLA Ops:
  0.0 98.9 %shard_map.109 = bf16[64,2048]{1,0:T(8,128)(2,1)S(1)} custom-call(bf16[64,256,4096]{2,1,0:T(8,128)(2,1)} %bitcast.1.k_hbm, bf16[64,256,4096]{2,1,0:T(8,128)(2,1)} %bitcast.3.v_hbm, bf16[64,2048]{1,0:T(8,128)(2,1)} %x_hbm.1, bf16[16,128]{1,0:T(8,128)(2,1)} %bitcast.8, bf16[2048,256]{1,0:T(8,128)(2,1)} %wq_hbm.1, bf16[256,2048]{1,0:T(8,128)(2,1)} %wo_hbm.1, ...), custom_call_target="tpu_custom_call" | custom-call | tf_op jit(solution)/shard_map/pallas_call | solution.py:312
  98.9 0.7 copy.13

commit v3 on v2

--- a/solution.py
+++ b/solution.py
@@ -25,6 +25,7 @@
     (60, (("project", 2),)),
     (64, (("project", 3), ("reduce2", 1), ("feed", 2), ("feed", 3), ("finish", 1), ("finish", 2), ("finish", 3))),
 )
+PIECES = 4
 MESH = pl.DeviceIdType.MESH
 F32, BF16 = jnp.float32, jnp.bfloat16
 
@@ -61,8 +62,12 @@
     (kbuf, vbuf, x_ref, ga, gm, table, wq, wo, wgu, wd, xf, hf, qf, seen, scores, ksem, vsem, wsem) = scratch[:18]
     chunks = len(CHUNKS)
     send_sem, recv_sem = scratch[18:20]
-    rest, bufs = list(scratch[20:]), []
+    last_sem = scratch[20]
+    rest, bufs, slots, used = list(scratch[21:]), [], [], 0
     for _, split in CHUNKS:
+        kinds = range(4) if split else (0, 2)
+        slots.append({kind: used + i for i, kind in enumerate(kinds)})
+        used += len(kinds)
         count = 6 if split else 2
         bufs.append(rest[:count])
         rest = rest[count:]
@@ -80,6 +85,14 @@
     def vcopy(s):
         slot = lax.rem(s, SLOTS)
         return pltpu.make_async_copy(v_hbm.at[s], vbuf.at[slot], vsem.at[slot])
+
+    def vpieces():
+        size = cache // PIECES
+        slot = (rows - 1) % SLOTS
+        return [
+            pltpu.make_async_copy(v_hbm.at[rows - 1, :, pl.ds(i * size, size)], vbuf.at[slot, :, pl.ds(i * size, size)], last_sem.at[i])
+            for i in range(PIECES)
+        ]
 
     small = [
         pltpu.make_async_copy(src, dst, wsem.at[i])
@@ -127,33 +140,39 @@
         query = jnp.where(own, jnp.broadcast_to(qf[pl.ds(s, 1), :], (8, width)), 0.0).astype(BF16)
         return dot(query, kbuf[lax.rem(s, SLOTS)])
 
-    def attend(s, wide):
+    def weigh(wide):
         scaled = wide * HEAD**-0.5
         e = jnp.exp(scaled - jnp.max(scaled, -1, keepdims=True))
-        weights = (e * (1.0 / jnp.sum(e, -1, keepdims=True))).astype(BF16)
-        out = dot_t(weights, vbuf[lax.rem(s, SLOTS)])
+        return (e * (1.0 / jnp.sum(e, -1, keepdims=True))).astype(BF16)
+
+    def keep(s, out):
         seen[pl.ds(s, 1), :] = jnp.sum(jnp.where(own, out, 0.0), 0, keepdims=True)
+
+    def attend(s, wide):
+        keep(s, dot_t(weigh(wide), vbuf[lax.rem(s, SLOTS)]))
 
     def send(kind, c, i, src, dst):
         return pltpu.make_async_remote_copy(
             src_ref=src,
             dst_ref=dst,
-            send_sem=send_sem.at[kind, c, i],
-            recv_sem=recv_sem.at[kind, c, me],
+            send_sem=send_sem.at[slots[c][kind]],
+            recv_sem=recv_sem.at[slots[c][kind]],
             device_id={"tp": peers[i]},
             device_id_type=MESH,
         )
 
+    def others(kind, c, src, dst):
+        return pltpu.make_async_remote_copy(
+            src_ref=src.at[pl.ds(0, n - 1)],
+            dst_ref=dst.at[pl.ds(0, n - 1)],
+            send_sem=send_sem.at[slots[c][kind]],
+            recv_sem=recv_sem.at[slots[c][kind]],
+            device_id={"tp": peers[0]},
+            device_id_type=MESH,
+        )
+
     def arrive(kind, c, buf):
-        for peer in peers:
-            pltpu.make_async_remote_copy(
-                src_ref=buf.at[peer],
-                dst_ref=buf.at[peer],
-                send_sem=send_sem.at[kind, c, 0],
-                recv_sem=recv_sem.at[kind, c, peer],
-                device_id={"tp": peer},
-                device_id_type=MESH,
-            ).wait_recv()
+        others(kind, c, buf, buf).wait_recv()
 
     def total(buf):
         out = buf[0].astype(F32)
@@ -205,19 +224,25 @@
         whole[me] = (before + total(landed)).astype(BF16)
         start(spread(2 * half + 1, c, whole))
 
-    def feed(c):
+    def states(c):
         if CHUNKS[c][1]:
             arrive(1, c, bufs[c][2])
-            h = joined(bufs[c][2])
-        else:
-            arrive(0, c, bufs[c][0])
-            h = (xf[parts[c], :] + total(bufs[c][0])).astype(BF16).astype(F32)
-            hf[parts[c], :] = h
+            return joined(bufs[c][2])
+        arrive(0, c, bufs[c][0])
+        h = (xf[parts[c], :] + total(bufs[c][0])).astype(BF16).astype(F32)
+        hf[parts[c], :] = h
+        return h
+
+    def feed(*group):
+        h = jnp.concatenate([states(c) for c in group], 0)
         b = normed(h, row_of(gm))
         both = dot(b, wgu[...])
         gate, up = both[:, :hidden], both[:, hidden:]
         product = (gate * (1.0 / (1.0 + jnp.exp(-gate))) * up).astype(BF16)
-        send_term(1, c, dot(product, wd[...]))
+        term, at = dot(product, wd[...]), 0
+        for c in group:
+            send_term(1, c, term[at : at + CHUNKS[c][0], :])
+            at += CHUNKS[c][0]
 
     def finish(c):
         if CHUNKS[c][1]:
@@ -244,36 +269,44 @@
         def _():
             kcopy(s + 1 + SLOTS).start()
 
-        @pl.when(s + SLOTS < rows)
+        @pl.when(s + SLOTS < rows - 1)
         def _():
             vcopy(s + SLOTS).start()
 
+        @pl.when(s + SLOTS == rows - 1)
+        def _():
+            start(vpieces())
+
         for row, names in EVENTS:
             if row < rows:
 
                 @pl.when(s == row - 1)
                 def _():
-                    for name, c in names:
-                        stages[name](c)
+                    for name, *group in names:
+                        stages[name](*group)
 
         return 0
 
     lax.fori_loop(0, rows - 1, step, 0)
-    vcopy(rows - 1).wait()
-    attend(rows - 1, scores[(rows - 1) % 2])
+    weights = weigh(scores[(rows - 1) % 2])
+    size = cache // PIECES
+    out = jnp.zeros((8, width), F32)
+    for i, copy in enumerate(vpieces()):
+        copy.wait()
+        out = out + dot_t(weights[:, i * size : (i + 1) * size], vbuf[(rows - 1) % SLOTS, :, i * size : (i + 1) * size])
+    keep(rows - 1, out)
     for row, names in EVENTS:
         if row == rows:
-            for name, c in names:
-                stages[name](c)
+            for name, *group in names:
+                stages[name](*group)
 
     for c in range(chunks):
         for half in range(2):
             if CHUNKS[c][1]:
-                copies = scatter(2 * half, c, *bufs[c][3 * half : 3 * half + 2]) + spread(2 * half + 1, c, bufs[c][3 * half + 2])
+                others(2 * half, c, bufs[c][3 * half], bufs[c][3 * half + 1]).wait_send()
+                others(2 * half + 1, c, bufs[c][3 * half + 2], bufs[c][3 * half + 2]).wait_send()
             else:
-                copies = spread(2 * half, c, bufs[c][half])
-            for copy in copies:
-                copy.wait_send()
+                others(2 * half, c, bufs[c][half], bufs[c][half]).wait_send()
 
 
 def solution(mesh):
@@ -284,7 +317,7 @@
         d, width, hidden = x.shape[1], heads * head, w_gate.shape[1]
         flat = lambda t: t.transpose(0, 2, 3, 1).reshape(rows, width, cache)
         table = jnp.asarray(turn_table(cache - 1, heads))
-        chunks = len(CHUNKS)
+        exchanges = sum(4 if split else 2 for _, split in CHUNKS)
         scratch = [
             pltpu.VMEM((SLOTS, width, cache), BF16),
             pltpu.VMEM((SLOTS, width, cache), BF16),
@@ -304,8 +337,9 @@
             pltpu.SemaphoreType.DMA((SLOTS,)),
             pltpu.SemaphoreType.DMA((SLOTS,)),
             pltpu.SemaphoreType.DMA((9,)),
-            pltpu.SemaphoreType.DMA((4, chunks, n - 1)),
-            pltpu.SemaphoreType.DMA((4, chunks, n)),
+            pltpu.SemaphoreType.DMA((exchanges,)),
+            pltpu.SemaphoreType.DMA((exchanges,)),
+            pltpu.SemaphoreType.DMA((PIECES,)),
         ]
         for size, split in CHUNKS:
             scratch += [pltpu.VMEM((n, size, d // n), BF16)] * 6 if split else [pltpu.VMEM((n, size, d), BF16)] * 2

time: 99.7 us -> 97.7 us (0.980)
  Pallas kernels: 98.9 us -> 96.9 us
    pallas_call x1, Pallas kernels: 98.9 us -> 96.9 us  [step(): pl.pallas_call(functools.partial(kernel, n), out_shape=pltpu.VMEM((rows,...]
where the time goes in v3:
time: 97.7 us; the launch traced here: 97.6 us
  Pallas kernels  96.9 us (99%)
    pallas_call x1, Pallas kernels, step(): pl.pallas_call(functools.partial(kernel, n), out_shape=pltpu.VMEM((rows,...  96.9 us

profile of v3, /device:TPU:0, one launch (start us, length us, event | category | flops | bytes accessed | tf_op | source)
XLA Modules:
  0.0 97.6 jit_solution(987256245577806715)
XLA Ops:
  0.0 96.9 %shard_map.109 = bf16[64,2048]{1,0:T(8,128)(2,1)S(1)} custom-call(bf16[64,256,4096]{2,1,0:T(8,128)(2,1)} %bitcast.1.k_hbm, bf16[64,256,4096]{2,1,0:T(8,128)(2,1)} %bitcast.3.v_hbm, bf16[64,2048]{1,0:T(8,128)(2,1)} %x_hbm.1, bf16[16,128]{1,0:T(8,128)(2,1)} %bitcast.8, bf16[2048,256]{1,0:T(8,128)(2,1)} %wq_hbm.1, bf16[256,2048]{1,0:T(8,128)(2,1)} %wo_hbm.1, ...), custom_call_target="tpu_custom_call" | custom-call | tf_op jit(solution)/shard_map/pallas_call | solution.py:346
  96.9 0.7 copy.13

commit v4 on v3

--- a/solution.py
+++ b/solution.py
@@ -12,18 +12,16 @@
 THETA = 10000
 EPS = 1e-6
 SLOTS = 8
-CHUNKS = ((32, True), (20, True), (8, False), (4, False))
+CHUNKS = ((40, True, True), (16, True, True), (4, False, False), (4, False, False))
 EVENTS = (
-    (32, (("project", 0),)),
-    (36, (("reduce1", 0),)),
-    (40, (("feed", 0),)),
-    (44, (("reduce2", 0),)),
-    (48, (("finish", 0),)),
-    (52, (("project", 1),)),
-    (54, (("reduce1", 1),)),
-    (58, (("feed", 1),)),
-    (60, (("project", 2),)),
-    (64, (("project", 3), ("reduce2", 1), ("feed", 2), ("feed", 3), ("finish", 1), ("finish", 2), ("finish", 3))),
+    (40, (("project", 0),)),
+    (44, (("reduce1", 0),)),
+    (48, (("feed", 0),)),
+    (52, (("reduce2", 0),)),
+    (56, (("project", 1),)),
+    (57, (("finish", 0),)),
+    (60, (("project", 2), ("reduce1", 1))),
+    (64, (("project", 3), ("feed", 1, 2), ("feed", 3), ("reduce2", 1), ("finish", 1), ("finish", 2), ("finish", 3))),
 )
 PIECES = 4
 MESH = pl.DeviceIdType.MESH
@@ -64,13 +62,15 @@
     send_sem, recv_sem = scratch[18:20]
     last_sem = scratch[20]
     rest, bufs, slots, used = list(scratch[21:]), [], [], 0
-    for _, split in CHUNKS:
-        kinds = range(4) if split else (0, 2)
-        slots.append({kind: used + i for i, kind in enumerate(kinds)})
-        used += len(kinds)
-        count = 6 if split else 2
-        bufs.append(rest[:count])
-        rest = rest[count:]
+    for _, *splits in CHUNKS:
+        bufs.append([])
+        slots.append({})
+        for half, split in enumerate(splits):
+            bufs[-1].append(rest[: 3 if split else 1])
+            rest = rest[3 if split else 1 :]
+            for kind in (2 * half, 2 * half + 1) if split else (2 * half,):
+                slots[-1][kind] = used
+                used += 1
     me = lax.axis_index("tp")
     peers = [lax.rem(me + i, n) for i in range(1, n)]
     if n == 8:
@@ -193,20 +193,20 @@
         for copy in copies:
             copy.start()
 
-    starts = [sum(size for size, _ in CHUNKS[:c]) for c in range(chunks)]
+    starts = [sum(chunk[0] for chunk in CHUNKS[:c]) for c in range(chunks)]
     parts = [slice(starts[c], starts[c] + CHUNKS[c][0]) for c in range(chunks)]
     tile = x_hbm.shape[1] // n
     mine = pl.ds(pl.multiple_of(me * tile, tile), tile)
 
     def send_term(half, c, term):
-        if CHUNKS[c][1]:
-            staged, landed = bufs[c][3 * half], bufs[c][3 * half + 1]
+        if CHUNKS[c][1 + half]:
+            staged, landed, _ = bufs[c][half]
             for i in range(n):
                 staged[i] = term[:, i * tile : (i + 1) * tile].astype(BF16)
             start(scatter(2 * half, c, staged, landed))
             landed[me] = staged[me]
         else:
-            buf = bufs[c][half]
+            (buf,) = bufs[c][half]
             buf[me] = term.astype(BF16)
             start(spread(2 * half, c, buf))
 
@@ -218,18 +218,24 @@
         send_term(0, c, dot(seen[parts[c], :].astype(BF16), wo[...]))
 
     def reduce(half, c):
-        landed, whole = bufs[c][3 * half + 1 : 3 * half + 3]
+        _, landed, whole = bufs[c][half]
         arrive(2 * half, c, landed)
-        before = xf[parts[c], mine] if half == 0 else bufs[c][2][me].astype(F32)
+        if half == 0:
+            before = xf[parts[c], mine]
+        elif CHUNKS[c][1]:
+            before = bufs[c][0][2][me].astype(F32)
+        else:
+            before = hf[parts[c], mine]
         whole[me] = (before + total(landed)).astype(BF16)
         start(spread(2 * half + 1, c, whole))
 
     def states(c):
         if CHUNKS[c][1]:
-            arrive(1, c, bufs[c][2])
-            return joined(bufs[c][2])
-        arrive(0, c, bufs[c][0])
-        h = (xf[parts[c], :] + total(bufs[c][0])).astype(BF16).astype(F32)
+            arrive(1, c, bufs[c][0][2])
+            return joined(bufs[c][0][2])
+        (buf,) = bufs[c][0]
+        arrive(0, c, buf)
+        h = (xf[parts[c], :] + total(buf)).astype(BF16).astype(F32)
         hf[parts[c], :] = h
         return h
 
@@ -245,12 +251,13 @@
             at += CHUNKS[c][0]
 
     def finish(c):
-        if CHUNKS[c][1]:
-            arrive(3, c, bufs[c][5])
-            y_ref[parts[c], :] = joined(bufs[c][5]).astype(BF16)
+        if CHUNKS[c][2]:
+            arrive(3, c, bufs[c][1][2])
+            y_ref[parts[c], :] = joined(bufs[c][1][2]).astype(BF16)
         else:
-            arrive(2, c, bufs[c][1])
-            y_ref[parts[c], :] = (hf[parts[c], :] + total(bufs[c][1])).astype(BF16)
+            (buf,) = bufs[c][1]
+            arrive(2, c, buf)
+            y_ref[parts[c], :] = (hf[parts[c], :] + total(buf)).astype(BF16)
 
     stages = {"project": project, "reduce1": functools.partial(reduce, 0), "feed": feed, "reduce2": functools.partial(reduce, 1), "finish": finish}
 
@@ -302,11 +309,10 @@
 
     for c in range(chunks):
         for half in range(2):
-            if CHUNKS[c][1]:
-                others(2 * half, c, bufs[c][3 * half], bufs[c][3 * half + 1]).wait_send()
-                others(2 * half + 1, c, bufs[c][3 * half + 2], bufs[c][3 * half + 2]).wait_send()
-            else:
-                others(2 * half, c, bufs[c][half], bufs[c][half]).wait_send()
+            own_buf, *more = bufs[c][half]
+            others(2 * half, c, own_buf, own_buf).wait_send()
+            if more:
+                others(2 * half + 1, c, more[1], more[1]).wait_send()
 
 
 def solution(mesh):
@@ -317,7 +323,7 @@
         d, width, hidden = x.shape[1], heads * head, w_gate.shape[1]
         flat = lambda t: t.transpose(0, 2, 3, 1).reshape(rows, width, cache)
         table = jnp.asarray(turn_table(cache - 1, heads))
-        exchanges = sum(4 if split else 2 for _, split in CHUNKS)
+        exchanges = sum(2 if split else 1 for _, *splits in CHUNKS for split in splits)
         scratch = [
             pltpu.VMEM((SLOTS, width, cache), BF16),
             pltpu.VMEM((SLOTS, width, cache), BF16),
@@ -341,8 +347,9 @@
             pltpu.SemaphoreType.DMA((exchanges,)),
             pltpu.SemaphoreType.DMA((PIECES,)),
         ]
-        for size, split in CHUNKS:
-            scratch += [pltpu.VMEM((n, size, d // n), BF16)] * 6 if split else [pltpu.VMEM((n, size, d), BF16)] * 2
+        for size, *splits in CHUNKS:
+            for split in splits:
+                scratch += [pltpu.VMEM((n, size, d // n), BF16)] * 3 if split else [pltpu.VMEM((n, size, d), BF16)]
         return pl.pallas_call(
             functools.partial(kernel, n),
             out_shape=pltpu.VMEM((rows, d), BF16),

time: 97.7 us -> 96.6 us (0.989)
  Pallas kernels: 96.9 us -> 95.8 us
    pallas_call x1, Pallas kernels: 96.9 us -> 95.8 us  [step(): pl.pallas_call(functools.partial(kernel, n), out_shape=pltpu.VMEM((rows,...]
where the time goes in v4:
time: 96.6 us; the launch traced here: 96.5 us
  Pallas kernels  95.8 us (99%)
    pallas_call x1, Pallas kernels, step(): pl.pallas_call(functools.partial(kernel, n), out_shape=pltpu.VMEM((rows,...  95.8 us

profile of v4, /device:TPU:0, one launch (start us, length us, event | category | flops | bytes accessed | tf_op | source)
XLA Modules:
  0.0 96.5 jit_solution(8596629681642951776)
XLA Ops:
  0.0 95.8 %shard_map.109 = bf16[64,2048]{1,0:T(8,128)(2,1)S(1)} custom-call(bf16[64,256,4096]{2,1,0:T(8,128)(2,1)} %bitcast.1.k_hbm, bf16[64,256,4096]{2,1,0:T(8,128)(2,1)} %bitcast.3.v_hbm, bf16[64,2048]{1,0:T(8,128)(2,1)} %x_hbm.1, bf16[16,128]{1,0:T(8,128)(2,1)} %bitcast.8, bf16[2048,256]{1,0:T(8,128)(2,1)} %wq_hbm.1, bf16[256,2048]{1,0:T(8,128)(2,1)} %wo_hbm.1, ...), custom_call_target="tpu_custom_call" | custom-call | tf_op jit(solution)/shard_map/pallas_call | solution.py:353
  95.8 0.7 copy.13

commit v5 on v4

--- a/solution.py
+++ b/solution.py
@@ -23,7 +23,7 @@
     (60, (("project", 2), ("reduce1", 1))),
     (64, (("project", 3), ("feed", 1, 2), ("feed", 3), ("reduce2", 1), ("finish", 1), ("finish", 2), ("finish", 3))),
 )
-PIECES = 4
+PIECES = 1
 MESH = pl.DeviceIdType.MESH
 F32, BF16 = jnp.float32, jnp.bfloat16
 
@@ -305,7 +305,10 @@
     for row, names in EVENTS:
         if row == rows:
             for name, *group in names:
-                stages[name](*group)
+                if name == "project":
+                    pl.when(me >= 0)(functools.partial(project, *group))
+                else:
+                    stages[name](*group)
 
     for c in range(chunks):
         for half in range(2):

time: 96.6 us -> 96 us (level)
  no operation moved by 1% of the time
where the time goes in v5:
time: 96 us; the launch traced here: 95.9 us
  Pallas kernels  95.2 us (99%)
    pallas_call x1, Pallas kernels, step(): pl.pallas_call(functools.partial(kernel, n), out_shape=pltpu.VMEM((rows,...  95.2 us

profile of v5, /device:TPU:0, one launch (start us, length us, event | category | flops | bytes accessed | tf_op | source)
XLA Modules:
  0.0 95.9 jit_solution(11253140384647067352)
XLA Ops:
  0.0 95.2 %shard_map.109 = bf16[64,2048]{1,0:T(8,128)(2,1)S(1)} custom-call(bf16[64,256,4096]{2,1,0:T(8,128)(2,1)} %bitcast.1.k_hbm, bf16[64,256,4096]{2,1,0:T(8,128)(2,1)} %bitcast.3.v_hbm, bf16[64,2048]{1,0:T(8,128)(2,1)} %x_hbm.1, bf16[16,128]{1,0:T(8,128)(2,1)} %bitcast.8, bf16[2048,256]{1,0:T(8,128)(2,1)} %wq_hbm.1, bf16[256,2048]{1,0:T(8,128)(2,1)} %wo_hbm.1, ...), custom_call_target="tpu_custom_call" | custom-call | tf_op jit(solution)/shard_map/pallas_call | solution.py:356
  95.2 0.7 copy.13
